TPU v7x, 256 devices: a whole 4x4x8 slice. The times are simulated.
256 devices in a mesh: vox: 64 (over x, z_lo, y, core), load: 4 (over z_hi).
Axes of the slice: x: 4, y: 4, z: 8 (z_hi: 4, z_lo: 2; z = z_hi * 2 + z_lo), core: 2. Of those that a mesh axis runs over, the one named last changes fastest.
Arguments:
- reduced_shape_matrix: bfloat16 [65536, 512], P('vox'), may hold values from -0.25 to 0.25
- young_modulus: float32 [65536], P('vox'), may hold values from 0.5 to 2
- work_stiffening_modulus: float32 [65536], P('vox'), may hold values from 0.2 to 2
- entry_flow_stress: float32 [65536], P('vox'), may hold values from 0.5 to 2
- dilation_factor: float32 [65536], P('vox'), may hold values from 0.5 to 2
- heat_difference: float32 [512], P('load'), may hold values from -4 to 4
- flowing_entry_flags: int32 [65536, 512], P('vox', 'load'), may hold values 0 or 1
- starting_permanent_deformation: float32 [65536, 512], P('vox', 'load'), may hold values from -3 to 3
- starting_weights: float32 [512, 512], P('vox', 'load'), may hold values from -5 to 5
- applied_reduced_vector: float32 [512, 512], P('vox', 'load'), may hold values from -768 to 768
- approx_tangent_inverse: float32 [512, 512], replicated, as said below
Outputs:
- final_mode_coefficients: float32 [512, 512], P('vox', 'load')
- strain_out: float32 [65536, 512], P('vox', 'load')
Inputs may be any that keep to these rules, and one draw needn't show every extreme that they name: `approx_tangent_inverse`: it has a positive diagonal.
All inputs are finite; a program needn't handle non-finite values. No bound on the sum of `flowing_entry_flags` on one device may be relied on, other than what follows from the above.
Results may differ from a plain program's by a relative error of at most 0.0013.
Values may be sent and summed in bfloat16 or wider, within the bound.
No kernel may reach another device: no remote copies, remote signals or barrier semaphores. Data moves between devices by JAX's collectives and lax.ppermute only.
A program may use at most 64 MiB of HBM per device.

v0:
```python
import jax
import jax.numpy as jnp
from jax import lax
from jax.sharding import Mesh
from jax.sharding import PartitionSpec as P

M = 512
ITERS = 3
VOX = ("vox_0", "vox_1", "vox_2", "vox_3")
VOX_LOAD = ("vox_0", "vox_1", "vox_2", "vox_3", "load")


def joined_along(pieces, dim):
    pieces = jnp.moveaxis(pieces, 0, dim)
    shape = pieces.shape
    return pieces.reshape(*shape[:dim], shape[dim] * shape[dim + 1], *shape[dim + 2 :])


def from_everyone(shard, axis):
    size = lax.axis_size(axis)
    return lax.all_to_all(
        jnp.broadcast_to(shard[None], (size, *shard.shape)), axis, 0, 0, tiled=True
    )


def collect(shard, axis, dim):
    return joined_along(from_everyone(shard, axis), dim)


def in_blocks(shard, dim, size):
    before, after = (shard.shape[:dim], shard.shape[dim + 1 :])
    return jnp.moveaxis(shard.reshape(*before, size, -1, *after), dim, 0)


def sum_at_owner(shard, axis, dim):
    size = lax.axis_size(axis)
    pieces = lax.all_to_all(in_blocks(shard, dim, size), axis, 0, 0, tiled=True)
    return jnp.sum(pieces, axis=0)


def over_axes(shard, axes):
    for axis in axes:
        shard = lax.psum(shard, axis)
    return shard


def shards(
    reduced_shape_matrix,
    young_modulus,
    work_stiffening_modulus,
    entry_flow_stress,
    dilation_factor,
    heat_difference,
    flowing_entry_flags,
    starting_permanent_deformation,
    starting_weights,
    applied_reduced_vector,
    approx_tangent_inverse,
):
    own_rows = starting_weights.shape[0]
    points = starting_weights.shape[1]
    load_point_total = points * lax.axis_size("load")
    plastic = starting_permanent_deformation
    active = flowing_entry_flags.astype(jnp.float32)
    modulus = young_modulus[:, None]
    harden = work_stiffening_modulus[:, None]
    yielded = entry_flow_stress[:, None]
    heating_history = dilation_factor[:, None] * heat_difference[None, :]
    xi_now = starting_weights
    my_precond = lax.dynamic_slice_in_dim(
        approx_tangent_inverse, lax.axis_index(VOX) * own_rows, own_rows, 0
    )
    for sweep in range(ITERS):
        xi_whole = collect(xi_now.astype(jnp.bfloat16), VOX, 0)
        strain = jnp.dot(reduced_shape_matrix, xi_whole, preferred_element_type=jnp.float32)
        trial = modulus * (strain - heating_history - plastic)
        excess = trial - yielded * jnp.tanh(trial / yielded)
        increment = active * excess / (modulus + harden)
        stress = (trial - modulus * increment).astype(jnp.bfloat16)
        stress, plastic = (stress, plastic + increment)
        partial_sum = lax.dot_general(
            reduced_shape_matrix,
            stress,
            (((0,), (0,)), ((), ())),
            preferred_element_type=jnp.float32,
        )
        resid = sum_at_owner(partial_sum, VOX, 0) - applied_reduced_vector
        resid_all = collect(resid, VOX, 0)
        delta = jnp.dot(my_precond, resid_all, precision=lax.Precision.HIGHEST)
        spread = over_axes(jnp.sum(delta * delta), VOX_LOAD) / (M * load_point_total)
        xi_now = xi_now - delta / (1.0 + spread)
    return (xi_now, plastic)


def solution(mesh):
    split = Mesh(
        mesh.devices.reshape(4, 2, 4, 2, mesh.shape["load"]),
        ("vox_0", "vox_1", "vox_2", "vox_3", "load"),
    )
    return jax.shard_map(
        shards,
        mesh=split,
        in_specs=(
            P(VOX, None),
            P(VOX),
            P(VOX),
            P(VOX),
            P(VOX),
            P("load"),
            P(VOX, "load"),
            P(VOX, "load"),
            P(VOX, "load"),
            P(VOX, "load"),
            P(),
        ),
        out_specs=(P(VOX, "load"), P(VOX, "load")),
        check_vma=False,
    )
```

profile of v0, /device:TPU:2, one launch (start us, length us, event | category | flops | bytes accessed | tf_op | source)
XLA Modules:
  0.0 264.1 jit_solution(17287310911029910719)
XLA Ops:
  0.6 0.0 copy-start
  0.6 0.8 convert_element_type.21
  1.4 0.7 broadcast_in_dim.12
  2.1 9.5 %all-to-all-start = ((bf16[64,8,128]{2,1,0:T(8,128)(2,1)}), bf16[64,8,128]{2,1,0:T(8,128)(2,1)S(1)}, u32[]{:S(2)}, u32[]{:S(2)}) async-start(bf16[64,8,128]{2,1,0:T(8,128)(2,1)} %broadcast_in_dim.12), calls=%async_computation | async-start | bytes 262144 | tf_op jit(solution)/shard_map/all_to_all | solution.py:21
  11.7 7.4 %all-to-all-done = bf16[64,8,128]{2,1,0:T(8,128)(2,1)S(1)} async-done(((bf16[64,8,128]{2,1,0:T(8,128)(2,1)}), bf16[64,8,128]{2,1,0:T(8,128)(2,1)S(1)}, u32[]{:S(2)}, u32[]{:S(2)}) %all-to-all-start) | async-done | bytes 131104 | tf_op jit(solution)/shard_map/all_to_all | solution.py:21
  19.1 1.5 fusion.1
  20.6 0.8 convolution_bitcast_fusion.4
  21.5 0.1 copy.15
  21.6 14.0 %all_to_all.45 = f32[64,8,128]{2,1,0:T(8,128)S(1)} all-to-all(f32[64,8,128]{2,1,0:T(8,128)S(1)} %bitcast.57), channel_id=1, replica_groups=mesh['vox_0'=4,'vox_1'=2,'vox_2'=4,'vox_3'=2,'load'=4] {'vox_0','vox_1',..., dimensions={0} | all-to-all | bytes 524288 | tf_op jit(solution)/shard_map/all_to_all | solution.py:37
  35.7 0.1 reduce_sum.54
  35.7 0.6 copy-done.2
  36.4 0.7 broadcast_in_dim.13
  37.1 5.7 %all-to-all-start.2 = ((f32[64,8,128]{2,1,0:T(8,128)}), f32[64,8,128]{2,1,0:T(8,128)S(1)}, u32[]{:S(2)}, u32[]{:S(2)}) async-start(f32[64,8,128]{2,1,0:T(8,128)} %broadcast_in_dim.13), calls=%async_computation.2 | async-start | bytes 524288 | tf_op jit(solution)/shard_map/all_to_all | solution.py:21
  42.8 8.8 %all-to-all-done.2 = f32[64,8,128]{2,1,0:T(8,128)S(1)} async-done(((f32[64,8,128]{2,1,0:T(8,128)}), f32[64,8,128]{2,1,0:T(8,128)S(1)}, u32[]{:S(2)}, u32[]{:S(2)}) %all-to-all-start.2) | async-done | bytes 262176 | tf_op jit(solution)/shard_map/all_to_all | solution.py:21
  51.6 1.6 multiply_reduce_fusion.2
  53.1 9.7 %psum.105 = f32[]{:T(128)} all-reduce(f32[]{:T(128)} %get-tuple-element.4), channel_id=1, replica_groups=mesh['vox_0'=4,'vox_1'=2,'vox_2'=4,'vox_3'=2,'load'=4] {'vox_0'}, use_global_device_ids=true, to_apply=%region_2.0 | all-reduce | flops 1 | bytes 8 | tf_op jit(solution)/shard_map/psum | solution.py:43
  62.8 5.5 %psum.106 = f32[]{:T(128)} all-reduce(f32[]{:T(128)} %psum.105), channel_id=1, replica_groups=mesh['vox_0'=4,'vox_1'=2,'vox_2'=4,'vox_3'=2,'load'=4] {'vox_1'}, use_global_device_ids=true, to_apply=%region_3.0 | all-reduce | flops 1 | bytes 8 | tf_op jit(solution)/shard_map/psum | solution.py:43
  68.4 9.5 %psum.107 = f32[]{:T(128)} all-reduce(f32[]{:T(128)} %psum.106), channel_id=1, replica_groups=mesh['vox_0'=4,'vox_1'=2,'vox_2'=4,'vox_3'=2,'load'=4] {'vox_2'}, use_global_device_ids=true, to_apply=%region_4.0 | all-reduce | flops 1 | bytes 8 | tf_op jit(solution)/shard_map/psum | solution.py:43
  77.9 3.1 %psum.108 = f32[]{:T(128)} all-reduce(f32[]{:T(128)} %psum.107), channel_id=1, replica_groups=mesh['vox_0'=4,'vox_1'=2,'vox_2'=4,'vox_3'=2,'load'=4] {'vox_3'}, use_global_device_ids=true, to_apply=%region_5.0 | all-reduce | flops 1 | bytes 8 | tf_op jit(solution)/shard_map/psum | solution.py:43
  81.0 14.6 %psum.109 = f32[]{:T(128)} all-reduce(f32[]{:T(128)} %psum.108), channel_id=1, replica_groups=mesh['vox_0'=4,'vox_1'=2,'vox_2'=4,'vox_3'=2,'load'=4] {'load'}, use_global_device_ids=true, to_apply=%region_6.0 | all-reduce | flops 1 | bytes 8 | tf_op jit(solution)/shard_map/psum | solution.py:43
  96.3 11.9 %all_to_all.46 = bf16[64,8,128]{2,1,0:T(8,128)(2,1)S(1)} all-to-all(bf16[64,8,128]{2,1,0:T(8,128)(2,1)S(1)} %broadcast_in_dim.14), channel_id=1, replica_groups=mesh['vox_0'=4,'vox_1'=2,'vox_2'=4,'vox_3'=2,'load'=4] {'vox_0','vox_1',..., dimensions={0} | all-to-all | bytes 262144 | tf_op jit(solution)/shard_map/all_to_all | solution.py:21
  108.2 0.7 fusion.7
  108.9 0.8 copy-done.10
  109.7 0.8 convolution_bitcast_fusion.3
  110.5 0.1 copy.17
  110.7 14.0 %all_to_all.47 = f32[64,8,128]{2,1,0:T(8,128)S(1)} all-to-all(f32[64,8,128]{2,1,0:T(8,128)S(1)} %bitcast.58), channel_id=1, replica_groups=mesh['vox_0'=4,'vox_1'=2,'vox_2'=4,'vox_3'=2,'load'=4] {'vox_0','vox_1',..., dimensions={0} | all-to-all | bytes 524288 | tf_op jit(solution)/shard_map/all_to_all | solution.py:37
  124.7 0.1 reduce_sum.56
  124.8 14.2 %all_to_all.48 = f32[64,8,128]{2,1,0:T(8,128)S(1)} all-to-all(f32[64,8,128]{2,1,0:T(8,128)S(1)} %broadcast_in_dim.15), channel_id=1, replica_groups=mesh['vox_0'=4,'vox_1'=2,'vox_2'=4,'vox_3'=2,'load'=4] {'vox_0','vox_1',..., dimensions={0} | all-to-all | bytes 524288 | tf_op jit(solution)/shard_map/all_to_all | solution.py:21
  139.0 1.6 multiply_reduce_fusion.1
  140.6 9.7 %psum.110 = f32[]{:T(128)} all-reduce(f32[]{:T(128)} %get-tuple-element.6), channel_id=1, replica_groups=mesh['vox_0'=4,'vox_1'=2,'vox_2'=4,'vox_3'=2,'load'=4] {'vox_0'}, use_global_device_ids=true, to_apply=%region_9.0 | all-reduce | flops 1 | bytes 8 | tf_op jit(solution)/shard_map/psum | solution.py:43
  150.3 5.5 %psum.111 = f32[]{:T(128)} all-reduce(f32[]{:T(128)} %psum.110), channel_id=1, replica_groups=mesh['vox_0'=4,'vox_1'=2,'vox_2'=4,'vox_3'=2,'load'=4] {'vox_1'}, use_global_device_ids=true, to_apply=%region_10.0 | all-reduce | flops 1 | bytes 8 | tf_op jit(solution)/shard_map/psum | solution.py:43
  155.8 9.5 %psum.112 = f32[]{:T(128)} all-reduce(f32[]{:T(128)} %psum.111), channel_id=1, replica_groups=mesh['vox_0'=4,'vox_1'=2,'vox_2'=4,'vox_3'=2,'load'=4] {'vox_2'}, use_global_device_ids=true, to_apply=%region_11.0 | all-reduce | flops 1 | bytes 8 | tf_op jit(solution)/shard_map/psum | solution.py:43
  165.3 3.1 %psum.113 = f32[]{:T(128)} all-reduce(f32[]{:T(128)} %psum.112), channel_id=1, replica_groups=mesh['vox_0'=4,'vox_1'=2,'vox_2'=4,'vox_3'=2,'load'=4] {'vox_3'}, use_global_device_ids=true, to_apply=%region_12.0 | all-reduce | flops 1 | bytes 8 | tf_op jit(solution)/shard_map/psum | solution.py:43
  168.4 10.7 %psum.114 = f32[]{:T(128)} all-reduce(f32[]{:T(128)} %psum.113), channel_id=1, replica_groups=mesh['vox_0'=4,'vox_1'=2,'vox_2'=4,'vox_3'=2,'load'=4] {'load'}, use_global_device_ids=true, to_apply=%region_13.0 | all-reduce | flops 1 | bytes 8 | tf_op jit(solution)/shard_map/psum | solution.py:43
  179.8 11.9 %all_to_all.49 = bf16[64,8,128]{2,1,0:T(8,128)(2,1)S(1)} all-to-all(bf16[64,8,128]{2,1,0:T(8,128)(2,1)S(1)} %broadcast_in_dim.16), channel_id=1, replica_groups=mesh['vox_0'=4,'vox_1'=2,'vox_2'=4,'vox_3'=2,'load'=4] {'vox_0','vox_1',..., dimensions={0} | all-to-all | bytes 262144 | tf_op jit(solution)/shard_map/all_to_all | solution.py:21
  191.7 1.8 add_add_fusion
  193.5 0.8 convolution_bitcast_fusion.2
  194.4 0.1 copy.19
  194.5 14.0 %all_to_all.50 = f32[64,8,128]{2,1,0:T(8,128)S(1)} all-to-all(f32[64,8,128]{2,1,0:T(8,128)S(1)} %bitcast.59), channel_id=1, replica_groups=mesh['vox_0'=4,'vox_1'=2,'vox_2'=4,'vox_3'=2,'load'=4] {'vox_0','vox_1',..., dimensions={0} | all-to-all | bytes 524288 | tf_op jit(solution)/shard_map/all_to_all | solution.py:37
  208.5 0.1 reduce_sum.58
  208.6 14.1 %all_to_all.51 = f32[64,8,128]{2,1,0:T(8,128)S(1)} all-to-all(f32[64,8,128]{2,1,0:T(8,128)S(1)} %broadcast_in_dim.17), channel_id=1, replica_groups=mesh['vox_0'=4,'vox_1'=2,'vox_2'=4,'vox_3'=2,'load'=4] {'vox_0','vox_1',..., dimensions={0} | all-to-all | bytes 524288 | tf_op jit(solution)/shard_map/all_to_all | solution.py:21
  222.7 1.6 multiply_reduce_fusion
  224.3 9.7 %psum.115 = f32[]{:T(128)} all-reduce(f32[]{:T(128)} %get-tuple-element.8), channel_id=1, replica_groups=mesh['vox_0'=4,'vox_1'=2,'vox_2'=4,'vox_3'=2,'load'=4] {'vox_0'}, use_global_device_ids=true, to_apply=%region_16.0 | all-reduce | flops 1 | bytes 8 | tf_op jit(solution)/shard_map/psum | solution.py:43
  234.0 5.5 %psum.116 = f32[]{:T(128)} all-reduce(f32[]{:T(128)} %psum.115), channel_id=1, replica_groups=mesh['vox_0'=4,'vox_1'=2,'vox_2'=4,'vox_3'=2,'load'=4] {'vox_1'}, use_global_device_ids=true, to_apply=%region_17.0 | all-reduce | flops 1 | bytes 8 | tf_op jit(solution)/shard_map/psum | solution.py:43
  239.5 9.5 %psum.117 = f32[]{:T(128)} all-reduce(f32[]{:T(128)} %psum.116), channel_id=1, replica_groups=mesh['vox_0'=4,'vox_1'=2,'vox_2'=4,'vox_3'=2,'load'=4] {'vox_2'}, use_global_device_ids=true, to_apply=%region_18.0 | all-reduce | flops 1 | bytes 8 | tf_op jit(solution)/shard_map/psum | solution.py:43
  249.0 3.1 %psum.118 = f32[]{:T(128)} all-reduce(f32[]{:T(128)} %psum.117), channel_id=1, replica_groups=mesh['vox_0'=4,'vox_1'=2,'vox_2'=4,'vox_3'=2,'load'=4] {'vox_3'}, use_global_device_ids=true, to_apply=%region_19.0 | all-reduce | flops 1 | bytes 8 | tf_op jit(solution)/shard_map/psum | solution.py:43
  252.1 10.7 %psum.119 = f32[]{:T(128)} all-reduce(f32[]{:T(128)} %psum.118), channel_id=1, replica_groups=mesh['vox_0'=4,'vox_1'=2,'vox_2'=4,'vox_3'=2,'load'=4] {'load'}, use_global_device_ids=true, to_apply=%region_20.0 | all-reduce | flops 1 | bytes 8 | tf_op jit(solution)/shard_map/psum | solution.py:43
  263.5 0.6 divide_subtract_fusion
  (31 shorter events, 0.2 us)
Async XLA Ops:
  0.6 18.5 %copy-start = (bf16[1024,512]{1,0:T(8,128)(2,1)S(1)}, bf16[1024,512]{1,0:T(8,128)(2,1)}, u32[]{:S(2)}) copy-start(bf16[1024,512]{1,0:T(8,128)(2,1)} %param.11) | copy-start | bytes 3145732
  2.1 9.5 %copy-start.4 = (f32[1024]{0:T(1024)S(1)}, f32[1024]{0:T(1024)}, u32[]{:S(2)}) copy-start(f32[1024]{0:T(1024)} %param.12) | copy-start | bytes 12292
  2.1 9.5 %copy-start.6 = (f32[1024]{0:T(1024)S(1)}, f32[1024]{0:T(1024)}, u32[]{:S(2)}) copy-start(f32[1024]{0:T(1024)} %param.13) | copy-start | bytes 12292
  2.1 17.0 %all-to-all-start = ((bf16[64,8,128]{2,1,0:T(8,128)(2,1)}), bf16[64,8,128]{2,1,0:T(8,128)(2,1)S(1)}, u32[]{:S(2)}, u32[]{:S(2)}) async-start(bf16[64,8,128]{2,1,0:T(8,128)(2,1)} %broadcast_in_dim.12), calls=%async_computation | async-start | bytes 262144 | tf_op jit(solution)/shard_map/all_to_all | solution.py:21
  11.6 7.5 %copy-start.5 = (f32[1024]{0:T(1024)S(1)}, f32[1024]{0:T(1024)}, u32[]{:S(2)}) copy-start(f32[1024]{0:T(1024)} %param.15) | copy-start | bytes 12292
  11.7 7.5 %copy-start.7 = (f32[128]{0:T(128)S(1)}, f32[128]{0:T(128)}, u32[]{:S(2)}) copy-start(f32[128]{0:T(128)} %param.16) | copy-start | bytes 1540
  11.7 8.9 %copy-start.8 = (s32[1024,128]{1,0:T(8,128)S(1)}, s32[1024,128]{1,0:T(8,128)}, u32[]{:S(2)}) copy-start(s32[1024,128]{1,0:T(8,128)} %param.17) | copy-start | bytes 1572868
  11.7 8.9 %copy-start.9 = (f32[1024]{0:T(1024)S(1)}, f32[1024]{0:T(1024)}, u32[]{:S(2)}) copy-start(f32[1024]{0:T(1024)} %param.14) | copy-start | bytes 12292
  35.7 0.7 copy-start.2
  37.1 71.1 %copy-start.1 = (f32[1024,128]{1,0:T(8,128)S(1)}, f32[1024,128]{1,0:T(8,128)}, u32[]{:S(2)}) copy-start(f32[1024,128]{1,0:T(8,128)} %param.18) | copy-start | bytes 1572868
  37.1 14.5 %all-to-all-start.2 = ((f32[64,8,128]{2,1,0:T(8,128)}), f32[64,8,128]{2,1,0:T(8,128)S(1)}, u32[]{:S(2)}, u32[]{:S(2)}) async-start(f32[64,8,128]{2,1,0:T(8,128)} %broadcast_in_dim.13), calls=%async_computation.2 | async-start | bytes 524288 | tf_op jit(solution)/shard_map/all_to_all | solution.py:21
  81.0 15.3 %copy-start.3 = (f32[8,128]{1,0:T(8,128)S(1)}, f32[8,128]{1,0:T(8,128)}, u32[]{:S(2)}) copy-start(f32[8,128]{1,0:T(8,128)} %param.19) | copy-start | bytes 12292
  108.9 0.8 copy-start.10
  124.8 66.9 %copy-start.11 = (f32[1024,128]{1,0:T(8,128)S(1)}, f32[1024,128]{1,0:T(8,128)}, u32[]{:S(2)}) copy-start(f32[1024,128]{1,0:T(8,128)} %copy-done.10) | copy-start | bytes 1572868
where the time goes:
time: 265 us; the launch traced here: 264 us
  blocking collectives  214 us (81%)
  waiting for transfers between devices  16.2 us (6%)
  starting transfers between devices  15.2 us (6%)
  matrix products  11.2 us (4%)
  local copies, waits for them, and re-layouts  3.32 us (1%)
  between operations  2.83 us (1%)
    psum x15, blocking collectives, over_axes(): shard = lax.psum(shard, axis)  119 us
    all_to_all x4, blocking collectives, from_everyone(): lax.all_to_all(jnp.broadcast_to(shard[None], (size, *shard.shape)), axis,...  52.2 us
    all_to_all x3, blocking collectives, sum_at_owner(): pieces = lax.all_to_all(in_blocks(shard, dim, size), axis, 0, 0, tiled=True)  42.1 us
    all_to_all x2, waiting for transfers between devices, from_everyone(): lax.all_to_all(jnp.broadcast_to(shard[None], (size, *shard.shape)), axis,...  16.2 us
    all_to_all x2, starting transfers between devices, from_everyone(): lax.all_to_all(jnp.broadcast_to(shard[None], (size, *shard.shape)), axis,...  15.2 us
  transfers between devices with their start and end apart: 2, of which 2 were waited for; matrix products, arithmetic and copies ran while one was open for 0% of the time, Pallas kernels for 0%

commit v1 on v0

--- a/solution.py
+++ b/solution.py
@@ -40,7 +40,7 @@
 
 def over_axes(shard, axes):
     for axis in axes:
-        shard = lax.psum(shard, axis)
+        shard = jnp.sum(lax.all_gather(shard, axis), axis=0)
     return shard
 
 

time: 265 us -> 289 us (1.091)
  blocking collectives: 214 us -> 190 us
  local copies, waits for them, and re-layouts: 3.32 us -> 27.3 us
  other arithmetic: 1.63 us -> 10.7 us
  waiting for transfers between devices: 16.2 us -> 24.4 us
  starting transfers between devices: 15.2 us -> 20.7 us
    psum x15 -> x0, blocking collectives: 119 us -> none  [over_axes(): shard = lax.psum(shard, axis)]
    unnamed x0 -> x15, blocking collectives: none -> 110 us
    unnamed x24 -> x69, local copies, waits for them, and re-layouts: 1.46 us -> 24.7 us
    all_to_all x3 -> x2, blocking collectives: 42.1 us -> 28.1 us  [sum_at_owner(): pieces = lax.all_to_all(in_blocks(shard, dim, size), axis, 0, 0, tiled=True)]
    reduce_sum x0 -> x15, other arithmetic: none -> 9.05 us  [over_axes(): shard = jnp.sum(lax.all_gather(shard, axis), axis=0)]
    all_to_all x0 -> x1, waiting for transfers between devices: none -> 8.83 us  [sum_at_owner(): pieces = lax.all_to_all(in_blocks(shard, dim, size), axis, 0, 0, tiled=True)]
    all_to_all x0 -> x1, starting transfers between devices: none -> 5.55 us  [sum_at_owner(): pieces = lax.all_to_all(in_blocks(shard, dim, size), axis, 0, 0, tiled=True)]
  transfers between devices with their start and end apart: 2 -> 3, of which waited for: 2 -> 3; matrix products, arithmetic and copies ran while one was open for 0% -> 0% of each run, Pallas kernels for 0% -> 0%
where the time goes in v1:
time: 289 us; the launch traced here: 288 us
  blocking collectives  190 us (66%)
  local copies, waits for them, and re-layouts  27.3 us (9%)
  waiting for transfers between devices  24.4 us (8%)
  starting transfers between devices  20.7 us (7%)
  matrix products  11.2 us (4%)
  other arithmetic  10.7 us (4%)
  between operations  2.91 us (1%)
    unnamed x15, blocking collectives  110 us
    all_to_all x4, blocking collectives, from_everyone(): lax.all_to_all(jnp.broadcast_to(shard[None], (size, *shard.shape)), axis,...  52.2 us
    all_to_all x2, blocking collectives, sum_at_owner(): pieces = lax.all_to_all(in_blocks(shard, dim, size), axis, 0, 0, tiled=True)  28.1 us
    unnamed x69, local copies, waits for them, and re-layouts  24.7 us
    all_to_all x2, waiting for transfers between devices, from_everyone(): lax.all_to_all(jnp.broadcast_to(shard[None], (size, *shard.shape)), axis,...  15.6 us
    all_to_all x2, starting transfers between devices, from_everyone(): lax.all_to_all(jnp.broadcast_to(shard[None], (size, *shard.shape)), axis,...  15.2 us
    reduce_sum x15, other arithmetic, over_axes(): shard = jnp.sum(lax.all_gather(shard, axis), axis=0)  9.05 us
    all_to_all x1, waiting for transfers between devices, sum_at_owner(): pieces = lax.all_to_all(in_blocks(shard, dim, size), axis, 0, 0, tiled=True)  8.83 us
  transfers between devices with their start and end apart: 3, of which 3 were waited for; matrix products, arithmetic and copies ran while one was open for 0% of the time, Pallas kernels for 0%

profile of v1, /device:TPU:2, one launch (start us, length us, event | category | flops | bytes accessed | tf_op | source)
XLA Modules:
  0.0 287.5 jit_solution(10634000545804459388)
XLA Ops:
  2.1 9.5 %all-to-all-start = ((bf16[64,8,128]{2,1,0:T(8,128)(2,1)}), bf16[64,8,128]{2,1,0:T(8,128)(2,1)S(1)}, u32[]{:S(2)}, u32[]{:S(2)}) async-start(bf16[64,8,128]{2,1,0:T(8,128)(2,1)} %broadcast_in_dim.12), calls=%async_computation | async-start | bytes 262144 | tf_op jit(solution)/shard_map/all_to_all | solution.py:21
  11.7 7.4 %all-to-all-done = bf16[64,8,128]{2,1,0:T(8,128)(2,1)S(1)} async-done(((bf16[64,8,128]{2,1,0:T(8,128)(2,1)}), bf16[64,8,128]{2,1,0:T(8,128)(2,1)S(1)}, u32[]{:S(2)}, u32[]{:S(2)}) %all-to-all-start) | async-done | bytes 131104 | tf_op jit(solution)/shard_map/all_to_all | solution.py:21
  19.1 1.5 fusion.1
  22.3 5.5 %all-to-all-start.1 = ((f32[64,8,128]{2,1,0:T(8,128)}), f32[64,8,128]{2,1,0:T(8,128)S(1)}, u32[]{:S(2)}, u32[]{:S(2)}) async-start(f32[64,8,128]{2,1,0:T(8,128)} %bitcast.2), calls=%async_computation.1 | async-start | bytes 524288 | tf_op jit(solution)/shard_map/all_to_all | solution.py:37
  27.9 8.8 %all-to-all-done.1 = f32[64,8,128]{2,1,0:T(8,128)S(1)} async-done(((f32[64,8,128]{2,1,0:T(8,128)}), f32[64,8,128]{2,1,0:T(8,128)S(1)}, u32[]{:S(2)}, u32[]{:S(2)}) %all-to-all-start.1) | async-done | bytes 262176 | tf_op jit(solution)/shard_map/all_to_all | solution.py:37
  37.6 5.7 %all-to-all-start.2 = ((f32[64,8,128]{2,1,0:T(8,128)}), f32[64,8,128]{2,1,0:T(8,128)S(1)}, u32[]{:S(2)}, u32[]{:S(2)}) async-start(f32[64,8,128]{2,1,0:T(8,128)} %broadcast_in_dim.13), calls=%async_computation.2 | async-start | bytes 524288 | tf_op jit(solution)/shard_map/all_to_all | solution.py:21
  44.0 8.1 %all-to-all-done.2 = f32[64,8,128]{2,1,0:T(8,128)S(1)} async-done(((f32[64,8,128]{2,1,0:T(8,128)}), f32[64,8,128]{2,1,0:T(8,128)S(1)}, u32[]{:S(2)}, u32[]{:S(2)}) %all-to-all-start.2) | async-done | bytes 262176 | tf_op jit(solution)/shard_map/all_to_all | solution.py:21
  52.1 1.6 multiply_reduce_fusion.2
  53.7 1.4 dynamic-update-slice
  55.7 9.1 %all-reduce = f32[4]{0:T(128)S(1)} all-reduce(f32[4]{0:T(128)S(1)} %dynamic-update-slice), channel_id=1, replica_groups=mesh['vox_0'=4,'vox_1'=2,'vox_2'=4,'vox_3'=2,'load'=4] {'vox_0'}, use_global_device_ids=true, to_apply=%add | all-reduce | flops 4 | bytes 32
  65.4 1.3 dynamic-update-slice.1
  67.3 4.9 %all-reduce.1 = f32[2]{0:T(128)S(1)} all-reduce(f32[2]{0:T(128)S(1)} %dynamic-update-slice.1), channel_id=1, replica_groups=mesh['vox_0'=4,'vox_1'=2,'vox_2'=4,'vox_3'=2,'load'=4] {'vox_1'}, use_global_device_ids=true, to_apply=%add.1 | all-reduce | flops 2 | bytes 16
  72.8 1.4 dynamic-update-slice.2
  74.8 8.9 %all-reduce.2 = f32[4]{0:T(128)S(1)} all-reduce(f32[4]{0:T(128)S(1)} %dynamic-update-slice.2), channel_id=1, replica_groups=mesh['vox_0'=4,'vox_1'=2,'vox_2'=4,'vox_3'=2,'load'=4] {'vox_2'}, use_global_device_ids=true, to_apply=%add.2 | all-reduce | flops 4 | bytes 32
  84.3 1.4 dynamic-update-slice.3
  86.3 2.4 all-reduce.3
  89.3 1.4 dynamic-update-slice.4
  90.7 14.0 %all-reduce.4 = f32[4]{0:T(128)S(1)} all-reduce(f32[4]{0:T(128)S(1)} %dynamic-update-slice.4), channel_id=1, replica_groups=mesh['vox_0'=4,'vox_1'=2,'vox_2'=4,'vox_3'=2,'load'=4] {'load'}, use_global_device_ids=true, to_apply=%add.4 | all-reduce | flops 4 | bytes 32
  106.0 11.9 %all_to_all.45 = bf16[64,8,128]{2,1,0:T(8,128)(2,1)S(1)} all-to-all(bf16[64,8,128]{2,1,0:T(8,128)(2,1)S(1)} %broadcast_in_dim.14), channel_id=1, replica_groups=mesh['vox_0'=4,'vox_1'=2,'vox_2'=4,'vox_3'=2,'load'=4] {'vox_0','vox_1',..., dimensions={0} | all-to-all | bytes 262144 | tf_op jit(solution)/shard_map/all_to_all | solution.py:21
  119.4 0.8 convolution_bitcast_fusion.3
  120.4 14.0 %all_to_all.49 = f32[64,8,128]{2,1,0:T(8,128)S(1)} all-to-all(f32[64,8,128]{2,1,0:T(8,128)S(1)} %bitcast.77), channel_id=1, replica_groups=mesh['vox_0'=4,'vox_1'=2,'vox_2'=4,'vox_3'=2,'load'=4] {'vox_0','vox_1',..., dimensions={0} | all-to-all | bytes 524288 | tf_op jit(solution)/shard_map/all_to_all | solution.py:37
  134.5 14.2 %all_to_all.46 = f32[64,8,128]{2,1,0:T(8,128)S(1)} all-to-all(f32[64,8,128]{2,1,0:T(8,128)S(1)} %broadcast_in_dim.15), channel_id=1, replica_groups=mesh['vox_0'=4,'vox_1'=2,'vox_2'=4,'vox_3'=2,'load'=4] {'vox_0','vox_1',..., dimensions={0} | all-to-all | bytes 524288 | tf_op jit(solution)/shard_map/all_to_all | solution.py:21
  148.8 1.6 multiply_reduce_fusion.1
  150.3 1.4 dynamic-update-slice.5
  151.8 9.1 %all-reduce.5 = f32[4]{0:T(128)S(1)} all-reduce(f32[4]{0:T(128)S(1)} %dynamic-update-slice.5), channel_id=1, replica_groups=mesh['vox_0'=4,'vox_1'=2,'vox_2'=4,'vox_3'=2,'load'=4] {'vox_0'}, use_global_device_ids=true, to_apply=%add.5 | all-reduce | flops 4 | bytes 32
  161.5 1.3 dynamic-update-slice.6
  162.8 4.9 %all-reduce.6 = f32[2]{0:T(128)S(1)} all-reduce(f32[2]{0:T(128)S(1)} %dynamic-update-slice.6), channel_id=1, replica_groups=mesh['vox_0'=4,'vox_1'=2,'vox_2'=4,'vox_3'=2,'load'=4] {'vox_1'}, use_global_device_ids=true, to_apply=%add.6 | all-reduce | flops 2 | bytes 16
  168.3 1.4 dynamic-update-slice.7
  169.7 8.9 %all-reduce.7 = f32[4]{0:T(128)S(1)} all-reduce(f32[4]{0:T(128)S(1)} %dynamic-update-slice.7), channel_id=1, replica_groups=mesh['vox_0'=4,'vox_1'=2,'vox_2'=4,'vox_3'=2,'load'=4] {'vox_2'}, use_global_device_ids=true, to_apply=%add.7 | all-reduce | flops 4 | bytes 32
  179.1 1.4 dynamic-update-slice.8
  180.5 2.4 all-reduce.8
  183.6 1.4 dynamic-update-slice.9
  184.9 10.2 %all-reduce.9 = f32[4]{0:T(128)S(1)} all-reduce(f32[4]{0:T(128)S(1)} %dynamic-update-slice.9), channel_id=1, replica_groups=mesh['vox_0'=4,'vox_1'=2,'vox_2'=4,'vox_3'=2,'load'=4] {'load'}, use_global_device_ids=true, to_apply=%add.9 | all-reduce | flops 4 | bytes 32
  196.5 11.9 %all_to_all.47 = bf16[64,8,128]{2,1,0:T(8,128)(2,1)S(1)} all-to-all(bf16[64,8,128]{2,1,0:T(8,128)(2,1)S(1)} %broadcast_in_dim.16), channel_id=1, replica_groups=mesh['vox_0'=4,'vox_1'=2,'vox_2'=4,'vox_3'=2,'load'=4] {'vox_0','vox_1',..., dimensions={0} | all-to-all | bytes 262144 | tf_op jit(solution)/shard_map/all_to_all | solution.py:21
  208.4 1.8 add_add_fusion
  211.2 14.0 %all_to_all.50 = f32[64,8,128]{2,1,0:T(8,128)S(1)} all-to-all(f32[64,8,128]{2,1,0:T(8,128)S(1)} %bitcast.78), channel_id=1, replica_groups=mesh['vox_0'=4,'vox_1'=2,'vox_2'=4,'vox_3'=2,'load'=4] {'vox_0','vox_1',..., dimensions={0} | all-to-all | bytes 524288 | tf_op jit(solution)/shard_map/all_to_all | solution.py:37
  225.3 14.1 %all_to_all.48 = f32[64,8,128]{2,1,0:T(8,128)S(1)} all-to-all(f32[64,8,128]{2,1,0:T(8,128)S(1)} %broadcast_in_dim.17), channel_id=1, replica_groups=mesh['vox_0'=4,'vox_1'=2,'vox_2'=4,'vox_3'=2,'load'=4] {'vox_0','vox_1',..., dimensions={0} | all-to-all | bytes 524288 | tf_op jit(solution)/shard_map/all_to_all | solution.py:21
  239.4 1.6 multiply_reduce_fusion
  241.0 1.4 dynamic-update-slice.10
  242.4 9.1 %all-reduce.10 = f32[4]{0:T(128)S(1)} all-reduce(f32[4]{0:T(128)S(1)} %dynamic-update-slice.10), channel_id=1, replica_groups=mesh['vox_0'=4,'vox_1'=2,'vox_2'=4,'vox_3'=2,'load'=4] {'vox_0'}, use_global_device_ids=true, to_apply=%add.10 | all-reduce | flops 4 | bytes 32
  252.1 1.3 dynamic-update-slice.11
  253.4 4.9 %all-reduce.11 = f32[2]{0:T(128)S(1)} all-reduce(f32[2]{0:T(128)S(1)} %dynamic-update-slice.11), channel_id=1, replica_groups=mesh['vox_0'=4,'vox_1'=2,'vox_2'=4,'vox_3'=2,'load'=4] {'vox_1'}, use_global_device_ids=true, to_apply=%add.11 | all-reduce | flops 2 | bytes 16
  258.9 1.4 dynamic-update-slice.12
  260.3 8.9 %all-reduce.12 = f32[4]{0:T(128)S(1)} all-reduce(f32[4]{0:T(128)S(1)} %dynamic-update-slice.12), channel_id=1, replica_groups=mesh['vox_0'=4,'vox_1'=2,'vox_2'=4,'vox_3'=2,'load'=4] {'vox_2'}, use_global_device_ids=true, to_apply=%add.12 | all-reduce | flops 4 | bytes 32
  269.8 1.4 dynamic-update-slice.13
  271.2 2.4 all-reduce.13
  274.2 1.4 dynamic-update-slice.14
  275.6 10.1 %all-reduce.14 = f32[4]{0:T(128)S(1)} all-reduce(f32[4]{0:T(128)S(1)} %dynamic-update-slice.14), channel_id=1, replica_groups=mesh['vox_0'=4,'vox_1'=2,'vox_2'=4,'vox_3'=2,'load'=4] {'load'}, use_global_device_ids=true, to_apply=%add.14 | all-reduce | flops 4 | bytes 32
  (92 shorter events, 19.6 us)
Async XLA Ops:
  0.6 18.5 %copy-start = (bf16[1024,512]{1,0:T(8,128)(2,1)S(1)}, bf16[1024,512]{1,0:T(8,128)(2,1)}, u32[]{:S(2)}) copy-start(bf16[1024,512]{1,0:T(8,128)(2,1)} %param.11) | copy-start | bytes 3145732
  2.1 9.5 %copy-start.4 = (f32[1024]{0:T(1024)S(1)}, f32[1024]{0:T(1024)}, u32[]{:S(2)}) copy-start(f32[1024]{0:T(1024)} %param.12) | copy-start | bytes 12292
  2.1 9.5 %copy-start.6 = (f32[1024]{0:T(1024)S(1)}, f32[1024]{0:T(1024)}, u32[]{:S(2)}) copy-start(f32[1024]{0:T(1024)} %param.13) | copy-start | bytes 12292
  2.1 17.0 %all-to-all-start = ((bf16[64,8,128]{2,1,0:T(8,128)(2,1)}), bf16[64,8,128]{2,1,0:T(8,128)(2,1)S(1)}, u32[]{:S(2)}, u32[]{:S(2)}) async-start(bf16[64,8,128]{2,1,0:T(8,128)(2,1)} %broadcast_in_dim.12), calls=%async_computation | async-start | bytes 262144 | tf_op jit(solution)/shard_map/all_to_all | solution.py:21
  11.6 7.5 %copy-start.5 = (f32[1024]{0:T(1024)S(1)}, f32[1024]{0:T(1024)}, u32[]{:S(2)}) copy-start(f32[1024]{0:T(1024)} %param.15) | copy-start | bytes 12292
  11.7 7.5 %copy-start.7 = (f32[128]{0:T(128)S(1)}, f32[128]{0:T(128)}, u32[]{:S(2)}) copy-start(f32[128]{0:T(128)} %param.16) | copy-start | bytes 1540
  11.7 9.0 %copy-start.8 = (s32[1024,128]{1,0:T(8,128)S(1)}, s32[1024,128]{1,0:T(8,128)}, u32[]{:S(2)}) copy-start(s32[1024,128]{1,0:T(8,128)} %param.17) | copy-start | bytes 1572868
  11.7 9.0 %copy-start.9 = (f32[1024]{0:T(1024)S(1)}, f32[1024]{0:T(1024)}, u32[]{:S(2)}) copy-start(f32[1024]{0:T(1024)} %param.14) | copy-start | bytes 12292
  22.3 14.4 %all-to-all-start.1 = ((f32[64,8,128]{2,1,0:T(8,128)}), f32[64,8,128]{2,1,0:T(8,128)S(1)}, u32[]{:S(2)}, u32[]{:S(2)}) async-start(f32[64,8,128]{2,1,0:T(8,128)} %bitcast.2), calls=%async_computation.1 | async-start | bytes 524288 | tf_op jit(solution)/shard_map/all_to_all | solution.py:37
  27.9 8.9 %copy-start.2 = (f32[8,128]{1,0:T(8,128)S(1)}, f32[8,128]{1,0:T(8,128)}, u32[]{:S(2)}) copy-start(f32[8,128]{1,0:T(8,128)} %param.20) | copy-start | bytes 12292
  37.5 5.7 %copy-start.14 = (u32[256]{0:T(256)S(1)}, u32[256]{0:T(256)}, u32[]{:S(2)}) copy-start(u32[256]{0:T(256)} %constant.41) | copy-start | bytes 3076
  37.5 17.6 %copy-start.13 = (u32[256]{0:T(256)S(1)}, u32[256]{0:T(256)}, u32[]{:S(2)}) copy-start(u32[256]{0:T(256)} %constant.46) | copy-start | bytes 3076
  37.6 29.1 %copy-start.12 = (u32[256]{0:T(256)S(1)}, u32[256]{0:T(256)}, u32[]{:S(2)}) copy-start(u32[256]{0:T(256)} %constant.51) | copy-start | bytes 3076
  37.6 36.6 %copy-start.11 = (u32[256]{0:T(256)S(1)}, u32[256]{0:T(256)}, u32[]{:S(2)}) copy-start(u32[256]{0:T(256)} %constant.56) | copy-start | bytes 3076
  37.6 48.1 %copy-start.10 = (u32[256]{0:T(256)S(1)}, u32[256]{0:T(256)}, u32[]{:S(2)}) copy-start(u32[256]{0:T(256)} %constant.61) | copy-start | bytes 3076
  37.6 68.4 %copy-start.3 = (f32[8,128]{1,0:T(8,128)S(1)}, f32[8,128]{1,0:T(8,128)}, u32[]{:S(2)}) copy-start(f32[8,128]{1,0:T(8,128)} %param.19) | copy-start | bytes 12292
  37.6 14.5 %all-to-all-start.2 = ((f32[64,8,128]{2,1,0:T(8,128)}), f32[64,8,128]{2,1,0:T(8,128)S(1)}, u32[]{:S(2)}, u32[]{:S(2)}) async-start(f32[64,8,128]{2,1,0:T(8,128)} %broadcast_in_dim.13), calls=%async_computation.2 | async-start | bytes 524288 | tf_op jit(solution)/shard_map/all_to_all | solution.py:21
  43.3 74.7 %copy-start.1 = (f32[1024,128]{1,0:T(8,128)S(1)}, f32[1024,128]{1,0:T(8,128)}, u32[]{:S(2)}) copy-start(f32[1024,128]{1,0:T(8,128)} %param.18) | copy-start | bytes 1572868
  118.6 0.8 copy-start.15
  134.5 73.8 %copy-start.16 = (f32[1024,128]{1,0:T(8,128)S(1)}, f32[1024,128]{1,0:T(8,128)}, u32[]{:S(2)}) copy-start(f32[1024,128]{1,0:T(8,128)} %copy-done.15) | copy-start | bytes 1572868
